TPU v7x, 32 devices: a whole 2x2x4 slice. The times are simulated.
32 devices in a mesh: dp: 16 (over z, y, core), tensor: 2 (over x).
Axes of the slice: x: 2, y: 2, z: 4, core: 2. Of those that a mesh axis runs over, the one named last changes fastest.
Arguments:
- attn_out: bfloat16 [12288, 2048], P('dp', 'tensor'), may hold values from -6 to 6
- out_proj_t: bfloat16 [4096, 2048], P(None, 'tensor'), may hold values from -0.09375 to 0.09375
- grad_out: bfloat16 [12288, 4096], P('dp', 'tensor'), may hold values from -6 to 6
- read_weights: float32 [12288, 16], P('dp'), may hold values from 0 to 0.0026041667
- memory_gate: float32 [256, 16], P('dp'), may hold values from -0.2 to 1
- write_pos: int32 [16, 16], P('dp'), may hold values from 0 to 767, as said below
Outputs:
- grad_attn_out: bfloat16 [12288, 2048], P('dp', 'tensor')
- grad_out_proj_t: float32 [4096, 2048], P('dp', 'tensor')
- grad_memory: float32 [256, 4096], P('dp', 'tensor')
Inputs may be any that keep to these rules, and one draw needn't show every extreme that they name: `write_pos`: the 16 positions of one segment are distinct.
All inputs are finite; a program needn't handle non-finite values.
Results may differ from a plain program's by a relative error of at most 0.0034.
Values may be sent and summed in bfloat16 or wider, within the bound.
A program may use at most 64 MiB of HBM per device.

v0:
```python
import jax
import jax.numpy as jnp
from jax import lax
from jax.sharding import PartitionSpec as P


def body(attn_out, out_proj_t, grad_out, read_weights, memory_gate, write_pos):
    high = lax.Precision.HIGHEST
    seg_len = attn_out.shape[0]
    slots = write_pos.shape[1]
    gate_at_step = memory_gate.T
    dy_cols = grad_out.astype(jnp.float32)
    local = jnp.dot(read_weights.T, dy_cols, precision=high, preferred_element_type=jnp.float32)
    all_gates, all_terms = (
        lax.all_gather(gate_at_step, "dp", axis=0, tiled=True),
        lax.all_gather(local, "dp", axis=0, tiled=True),
    )
    count = lax.axis_size("dp")
    mine = lax.axis_index("dp")

    def sweep(step, carry):
        which = (count - 1 - step).astype(jnp.int32)
        gate = lax.dynamic_slice_in_dim(all_gates, which * slots, slots, 0)
        term = lax.dynamic_slice_in_dim(all_terms, which * slots, slots, 0)
        fresh = jnp.dot(gate, carry, precision=high, preferred_element_type=jnp.float32) + term
        return jnp.where(which > mine, fresh, carry)

    after = lax.fori_loop(0, count, sweep, jnp.zeros_like(local))
    grad_memory = (
        jnp.dot(gate_at_step, after, precision=high, preferred_element_type=jnp.float32) + local
    )
    places = jnp.arange(seg_len, dtype=jnp.int32)
    onehot = (places[:, None] == write_pos[0][None, :]).astype(jnp.float32)
    written = jnp.dot(onehot, after, precision=high, preferred_element_type=jnp.float32)
    grad_z = (dy_cols + written).astype(jnp.bfloat16)
    full_z = lax.all_gather(grad_z, "tensor", axis=1, tiled=True)
    grad_attn = jnp.dot(full_z, out_proj_t, preferred_element_type=jnp.float32).astype(jnp.bfloat16)
    term = lax.dot_general(
        full_z, attn_out, (((0,), (0,)), ((), ())), preferred_element_type=jnp.float32
    )
    grad_weight = lax.psum_scatter(term, "dp", scatter_dimension=0, tiled=True)
    return (grad_attn, grad_weight, grad_memory)


def solution(mesh):
    return jax.shard_map(
        body,
        mesh=mesh,
        in_specs=(
            P("dp", "tensor"),
            P(None, "tensor"),
            P("dp", "tensor"),
            P("dp", None),
            P("dp", None),
            P("dp", None),
        ),
        out_specs=(P("dp", "tensor"), P("dp", "tensor"), P("dp", "tensor")),
        check_vma=False,
    )
```

profile of v0, /device:TPU:25, one launch (start us, length us, event | category | flops | bytes accessed | tf_op | source)
XLA Modules:
  0.0 353.9 jit_solution(3340920916491173491)
XLA Ops:
  7.2 0.0 copy-start
  7.2 0.0 copy-start.3
  7.2 0.0 all-gather.3.cloned.1.call-start
  7.2 4.0 %fusion.9 = f32[16,2048]{1,0:T(8,128)} fusion(f32[768,16]{0,1:T(8,128)} %param.11, bf16[768,2048]{1,0:T(8,128)(2,1)} %param.10), kind=kOutput, calls=%fused_computation.14 | convolution fusion | flops 301989888 | bytes 3325952 | tf_op jit(solution)/shard_map/dot_general | solution.py:13
  11.3 0.0 all-gather.3.cloned.1.call-update
  11.3 0.0 all-gather.5.cloned.1.call-start
  11.3 0.8 copy.9
  12.1 17.8 %all_gather.9 = f32[256,16]{1,0:T(8,128)S(1)} all-gather(f32[16,16]{1,0:T(8,128)S(1)} %bitcast.15), channel_id=1, replica_groups=mesh['dp'=16,'tensor'=2] {'dp'}, dimensions={0}, use_global_device_ids=true | all-gather | bytes 17408 | tf_op jit(solution)/shard_map/all_gather | solution.py:15
  29.9 23.0 %all-gather.3.cloned.1.call-done = f32[256,2048]{1,0:T(8,128)} async-done(((f32[16,2048]{1,0:T(8,128)}), f32[256,2048]{1,0:T(8,128)}) %all-gather.3.cloned.1.call-update) | async-done | bytes 2097168 | tf_op jit(solution)/shard_map/all_gather | solution.py:16
  52.9 19.5 %while.14 = (s32[]{:T(128)}, f32[16,2048]{1,0:T(8,128)S(1)}, s32[]{:T(128)}, f32[256,16]{1,0:T(8,128)S(1)}, f32[256,2048]{1,0:T(8,128)}, /*index=5*/s32[]{:T(128)}, s32[]{:T(128)}, s32[]{:T(128)}, s32[]{:T(128)}, s32[]{:T(128)}) while((s32[]{:T(128)}, f32[16,2048]{1,0:T(8,128)S(1)}, s32[]{:T(128)}, f32[256,16]{1,0:T(8,128)S(1)}, ...), condition=%wide.region_1.2_spmd.clone, body=%wide.region_0.1_spmd.clone.sunk | while | flops 6422537 | bytes 797361 | solution.py:28
  52.9 1.2 fusion.25
  54.2 1.2 fusion.25
  55.4 1.2 fusion.25
  56.6 1.2 fusion.25
  57.8 1.2 fusion.25
  59.0 1.2 fusion.25
  60.3 1.2 fusion.25
  61.5 1.2 fusion.25
  62.7 1.2 fusion.25
  63.9 1.2 fusion.25
  65.2 1.2 fusion.25
  66.4 1.2 fusion.25
  67.6 1.2 fusion.25
  68.8 1.2 fusion.25
  70.1 1.2 fusion.25
  71.3 1.2 fusion.25
  72.5 0.0 copy-done.3
  72.5 5.6 %add_convert_fusion = bf16[768,2048]{1,0:T(8,128)(2,1)} fusion(bf16[768,2048]{1,0:T(8,128)(2,1)} %param.10, f32[16,2048]{1,0:T(8,128)S(1)} %get-tuple-element.97, s32[16]{0:T(128)S(1)} %bitcast.16), kind=kOutput, calls=%fused_computation.8 | convolution fusion | flops 306720768 | bytes 6422592 | tf_op jit(solution)/shard_map/dot_general | solution.py:34
  78.0 0.0 all-gather.5.cloned.1.call-update
  78.1 0.0 reduce-scatter.2.cloned.1.call-start
  78.1 79.9 %all-gather.5.cloned.1.call-done = bf16[768,4096]{1,0:T(8,128)(2,1)} async-done(((bf16[768,2048]{1,0:T(8,128)(2,1)}), bf16[768,4096]{1,0:T(8,128)(2,1)}) %all-gather.5.cloned.1.call-update) | async-done | bytes 6291472 | tf_op jit(solution)/shard_map/all_gather | solution.py:36
  158.0 0.0 copy-done
  158.0 13.0 %fusion.10 = f32[4096,1024]{1,0:T(8,128)} fusion(bf16[768,4096]{1,0:T(8,128)(2,1)} %all-gather.5.cloned.1.call-done, bf16[768,1024]{1,0:T(8,128)(2,1)S(1)} %copy-done), kind=kOutput, calls=%fused_computation.15 | convolution fusion | flops 6442450944 | bytes 24641536 | tf_op jit(solution)/shard_map/dot_general | solution.py:38
  171.0 0.0 copy-start.1
  171.0 0.0 copy-start.2
  171.0 0.0 reduce-scatter.2.cloned.1.call-update
  171.1 0.9 copy-done.1
  171.9 0.0 copy-done.2
  171.9 1.0 fusion.7
  172.9 12.1 %convolution_convert_fusion = bf16[768,1024]{1,0:T(8,128)(2,1)} fusion(bf16[768,4096]{1,0:T(8,128)(2,1)} %all-gather.5.cloned.1.call-done, bf16[4096,1024]{1,0:T(8,128)(2,1)} %param.9), kind=kOutput, calls=%fused_computation.11 | convolution fusion | flops 6443237376 | bytes 16252928 | tf_op jit(solution)/shard_map/dot_general | solution.py:37
  185.0 162.4 %reduce-scatter.2.cloned.1.call-done = f32[256,1024]{1,0:T(8,128)} async-done(((f32[4096,1024]{1,0:T(8,128)}), f32[256,1024]{1,0:T(8,128)}) %reduce-scatter.2.cloned.1.call-update) | async-done | bytes 1048592 | tf_op jit(solution)/shard_map/reduce_scatter | solution.py:41
  (17 shorter events, 0.2 us)
Async XLA Ops:
  7.2 150.8 %copy-start = (bf16[768,1024]{1,0:T(8,128)(2,1)S(1)}, bf16[768,1024]{1,0:T(8,128)(2,1)}, u32[]{:S(2)}) copy-start(bf16[768,1024]{1,0:T(8,128)(2,1)} %param.8) | copy-start | bytes 4718596
  7.2 65.3 %copy-start.3 = (s32[1,16]{1,0:T(1,128)S(1)}, s32[1,16]{1,0:T(1,128)}, u32[]{:S(2)}) copy-start(s32[1,16]{1,0:T(1,128)} %param.13) | copy-start | bytes 196
  7.2 45.7 %all-gather.3.cloned.1.call-start = ((), (), s32[]{:S(2)}) async-start(), calls=%async_computation.1 | async-start | bytes 2228224 | tf_op jit(solution)/shard_map/all_gather | solution.py:16
  11.3 146.7 %all-gather.5.cloned.1.call-start = ((), (), s32[]{:S(2)}) async-start(), calls=%async_computation.2 | async-start | bytes 9437184 | tf_op jit(solution)/shard_map/all_gather | solution.py:36
  78.1 269.3 %reduce-scatter.2.cloned.1.call-start = ((), (), s32[]{:S(2)}) async-start(), calls=%async_computation.3 | async-start | bytes 17825792 | tf_op jit(solution)/shard_map/reduce_scatter | solution.py:41
  171.0 0.9 copy-start.1
  171.0 0.9 copy-start.2
Sparse Core Ops, SparseCore 0:
  11.4 41.4 all-gather.2
  78.2 79.7 all-gather.4
  171.2 176.1 reduce-scatter.1
where the time goes:
time: 358 us; the launch traced here: 354 us
  waiting for transfers between devices  265 us (74%)
  matrix products  54.3 us (15%)
  blocking collectives  17.8 us (5%)
  between operations  13.8 us (4%)
    reduce_scatter x1, waiting for transfers between devices, body(): grad_weight = lax.psum_scatter(term, 'dp', scatter_dimension=0, tiled=True)  162 us
    all_gather x1, waiting for transfers between devices, body(): full_z = lax.all_gather(grad_z, 'tensor', axis=1, tiled=True)  79.9 us
    all_gather x1, waiting for transfers between devices, body(): lax.all_gather(local, 'dp', axis=0, tiled=True)  23 us
    dot_general x16, matrix products, sweep(): jnp.dot(gate, carry, precision=high, preferred_element_type=jnp.float32)  18.7 us
    all_gather x1, blocking collectives, body(): lax.all_gather(gate_at_step, 'dp', axis=0, tiled=True)  17.8 us
    dot_general x1, matrix products, body(): lax.dot_general(full_z, attn_out, (((0,), (0,)), ((), ())), preferred_ele...  13 us
    dot_general x1, matrix products, body(): jnp.dot(full_z, out_proj_t, preferred_element_type=jnp.float32)  12.1 us
  transfers between devices with their start and end apart: 3, of which 3 were waited for; matrix products, arithmetic and copies ran while one was open for 4% of the time, Pallas kernels for 0%

commit v1 on v0

--- a/solution.py
+++ b/solution.py
@@ -1,10 +1,337 @@
+import functools
+
 import jax
 import jax.numpy as jnp
 from jax import lax
+from jax.experimental import pallas as pl
+from jax.experimental.pallas import tpu as pltpu
 from jax.sharding import PartitionSpec as P
 
-
-def body(attn_out, out_proj_t, grad_out, read_weights, memory_gate, write_pos):
+MESH = pl.DeviceIdType.MESH
+F32 = jnp.float32
+BF16 = jnp.bfloat16
+
+
+def split3(a):
+    hi = a.astype(BF16)
+    rest = a - hi.astype(F32)
+    mid = rest.astype(BF16)
+    low = (rest - mid.astype(F32)).astype(BF16)
+    return jnp.concatenate([hi, mid, low], axis=0)
+
+
+def tdot(a, b):
+    return lax.dot_general(a, b, (((0,), (0,)), ((), ())), preferred_element_type=F32)
+
+
+def kernel(
+    n, attn, w_hbm, g, rwt, gate, wpos, out_attn, out_w, out_mem,
+    w, attn_p, gx, za, zb, zp, acc, onehot, local, after, after_x,
+    lsend, lrecv, asend, arecv, ysend, yrecv, kept, zsend, zrecv, mine,
+    w_sem, x_s, x_r, l_s, l_r, a_s, a_r, ax_s, ax_r, t_s, t_r, p_s, p_r, y_s, y_r, z_s, z_r,
+):
+    d = lax.axis_index("dp")
+    t = lax.axis_index("tensor")
+    c = lax.rem(d, 2)
+    y = lax.rem(d // 2, 2)
+    z = d // 4
+    nz = n // 4
+    seg, half = g.shape
+    hd = attn.shape[1]
+    slots = rwt.shape[0]
+    bw = 2 * half // n
+    lw = half // n
+    zh = nz // 2
+    nq = 2 * zh
+    partner = (d + 1 - 2 * c, t)
+    xpeer = (d, 1 - t)
+    ypeer = (d + 2 - 4 * y, t)
+    tile = 256
+
+    def remote(src, dst, ss, rs, dev):
+        return pltpu.make_async_remote_copy(
+            src_ref=src, dst_ref=dst, send_sem=ss, recv_sem=rs, device_id=dev, device_id_type=MESH
+        )
+
+    def peer(o):
+        return lax.rem(d + o, n)
+
+    barrier = pltpu.get_barrier_semaphore()
+    for o in range(1, n):
+        pl.semaphore_signal(barrier, inc=1, device_id=(peer(o), t), device_id_type=MESH)
+    pl.semaphore_signal(barrier, inc=1, device_id=xpeer, device_id_type=MESH)
+
+    wcopy = pltpu.make_async_copy(w_hbm, w, w_sem)
+    wcopy.start()
+    pl.semaphore_wait(barrier, n)
+
+    def place(q):
+        zz = q // 2
+        yd = 1 - y if q % 2 == 0 else y
+        return zz, yd, 2 * zz + yd
+
+    def cols(q, par):
+        return pl.ds(pl.multiple_of((2 * place(q)[2] + par) * bw, bw), bw)
+
+    def pair_cols(q):
+        return pl.ds(pl.multiple_of(2 * place(q)[2] * bw, 2 * bw), 2 * bw)
+
+    xcopies = []
+    for q in range(nq):
+        for k in range(2):
+            par = 1 - c if k == 0 else c
+            i = 2 * q + k
+            xcopies.append(
+                remote(g.at[:, cols(q, par)], gx.at[:, cols(q, par)], x_s.at[i], x_r.at[i], xpeer)
+            )
+    early = 3
+    for copy in xcopies[:early]:
+        copy.start()
+    tcopy = remote(attn, attn_p, t_s, t_r, partner)
+    tcopy.start()
+
+    three = split3(rwt[...])
+
+    def local_step(i, _):
+        at = pl.ds(pl.multiple_of(i * tile, tile), tile)
+        r = jnp.dot(three, g[:, at], preferred_element_type=F32)
+        local[:, at] = r[:slots] + r[slots : 2 * slots] + r[2 * slots :]
+        return 0
+
+    lax.fori_loop(0, half // tile, local_step, 0)
+
+    def msg(o):
+        return local[:, pl.ds(pl.multiple_of(peer(o) * lw, lw), lw)]
+
+    lrecv[0, :slots, :] = msg(0)
+    lrecv[0, slots:, :] = gate[...]
+    lcopies = []
+    for o in range(1, n):
+        lsend[o, :slots, :] = msg(o)
+        lsend[o, slots:, :] = gate[...]
+        lcopies.append(remote(lsend.at[o], lrecv.at[o], l_s.at[o], l_r.at[o], (peer(o), t)))
+    for copy in lcopies:
+        copy.start()
+
+    place_of = lax.broadcasted_iota(jnp.int32, (seg, 3 * slots), 0)
+    onehot[...] = jnp.where(place_of == wpos[...], 1.0, 0.0).astype(BF16)
+    for copy in lcopies:
+        copy.wait_recv()
+
+    def sweep(i, carry):
+        s = n - 1 - i
+        slot = lax.rem(d - s + n, n)
+        target = lax.rem(s - d + n, n)
+        asend[target, :slots, :] = carry
+        m = lrecv[slot]
+        fresh = m[:slots]
+        for k in range(slots):
+            fresh = fresh + m[slots:, k : k + 1] * carry[k : k + 1, :]
+        asend[target, slots:, :] = fresh
+        return fresh
+
+    lax.fori_loop(0, n, sweep, jnp.zeros((slots, lw), F32))
+    acopies = []
+    for o in range(1, n):
+        acopies.append(remote(asend.at[o], arecv.at[o], a_s.at[o], a_r.at[o], (peer(o), t)))
+    for copy in acopies:
+        copy.start()
+    for copy in acopies:
+        copy.wait_recv()
+    for o in range(n):
+        src = lax.rem(d - o + n, n)
+        at = pl.ds(pl.multiple_of(src * lw, lw), lw)
+        m = asend[0] if o == 0 else arecv[o]
+        after[:, at] = m[:slots]
+        out_mem[:, at] = m[slots:]
+    axcopy = remote(after, after_x, ax_s, ax_r, xpeer)
+    axcopy.start()
+    for copy in xcopies[early:]:
+        copy.start()
+
+    def fix(src, aft, dst, at):
+        written = jnp.dot(onehot[...], split3(aft[:, at]), preferred_element_type=F32)
+        dst[:, at] = (src[:, at].astype(F32) + written).astype(BF16)
+
+    pcopies = []
+
+    def to_partner(zr, q, i):
+        copy = remote(zr.at[:, cols(q, 1 - c)], zp.at[i], p_s.at[i], p_r.at[i], partner)
+        copy.start()
+        pcopies.append(copy)
+
+    ncopies = []
+    ycopies = {}
+
+    def grad_block(zr, q, i, first):
+        pcopies[i].wait_recv()
+        if first:
+            tcopy.wait_recv()
+        slot = i // 2
+
+        def step(m, _):
+            at = pl.ds(pl.multiple_of(m * tile, tile), tile)
+            r = tdot(zr[:, cols(q, c)], attn[:, at]) + tdot(zp[i], attn_p[:, at])
+            if q % 2 == 0:
+                ysend[slot, :, at] = r.astype(BF16)
+            else:
+                kept[slot, :, at] = r
+            return 0
+
+        lax.fori_loop(0, hd // tile, step, 0)
+        if q % 2 == 0:
+            copy = remote(ysend.at[slot], yrecv.at[slot], y_s.at[slot], y_r.at[slot], ypeer)
+            copy.start()
+            ycopies[slot] = copy
+
+    def to_owner(h, q, i):
+        slot = i // 2
+        zd = zh * h + place(q)[0]
+        ycopies[slot].wait_recv()
+        own = zd == z
+
+        @pl.when(own)
+        def _():
+            mine[...] = kept[slot] + yrecv[slot].astype(F32)
+
+        @pl.when(jnp.logical_not(own))
+        def _():
+            o = lax.rem(zd - z + nz, nz)
+            zsend[slot] = (kept[slot] + yrecv[slot].astype(F32)).astype(BF16)
+            remote(
+                zsend.at[slot], zrecv.at[o], z_s.at[slot], z_r.at[o], (zd * 4 + 2 * y + c, t)
+            ).start()
+
+        ncopies.append((own, slot, zd))
+
+    for q in range(nq):
+        fix(g, after, za, cols(q, 1 - c))
+        to_partner(za, q, q)
+        fix(g, after, za, cols(q, c))
+    for q in range(nq):
+        grad_block(za, q, q, q == 0)
+    wcopy.wait()
+
+    def own_step(m, _):
+        at = pl.ds(pl.multiple_of(m * tile, tile), tile)
+        rows = pl.ds(pl.multiple_of(t * half, half), half)
+        acc[:, at] = jnp.dot(za[...], w[rows, at], preferred_element_type=F32)
+        return 0
+
+    lax.fori_loop(0, hd // tile, own_step, 0)
+    for q in range(1, nq, 2):
+        to_owner(t, q, q)
+
+    axcopy.wait_recv()
+    for q in range(nq):
+        i = nq + q
+        xcopies[2 * q].wait_recv()
+        fix(gx, after_x, zb, cols(q, 1 - c))
+        to_partner(zb, q, i)
+        xcopies[2 * q + 1].wait_recv()
+        fix(gx, after_x, zb, cols(q, c))
+        grad_block(zb, q, i, False)
+
+        def other_step(m, _, q=q):
+            at = pl.ds(pl.multiple_of(m * tile, tile), tile)
+            rows = pl.ds(
+                pl.multiple_of((1 - t) * half + 2 * place(q)[2] * bw, 2 * bw), 2 * bw
+            )
+            r = acc[:, at] + jnp.dot(zb[:, pair_cols(q)], w[rows, at], preferred_element_type=F32)
+            if q == nq - 1:
+                out_attn[:, at] = r.astype(BF16)
+            else:
+                acc[:, at] = r
+            return 0
+
+        if q % 2 == 1:
+            to_owner(1 - t, q, i)
+        lax.fori_loop(0, hd // tile, other_step, 0)
+
+    total = mine[...]
+    for o in range(1, nz):
+        remote(zrecv.at[o], zrecv.at[o], z_s.at[0], z_r.at[o], ypeer).wait_recv()
+        total = total + zrecv[o].astype(F32)
+    out_w[...] = total
+
+    for copy in xcopies + [tcopy, axcopy] + lcopies + acopies + pcopies + list(ycopies.values()):
+        copy.wait_send()
+    for own, slot, zd in ncopies:
+
+        @pl.when(jnp.logical_not(own))
+        def _():
+            remote(zsend.at[slot], zrecv.at[0], z_s.at[slot], z_r.at[0], ypeer).wait_send()
+
+
+def fused(n, attn_out, out_proj_t, grad_out, read_weights, memory_gate, write_pos):
+    seg, half = grad_out.shape
+    hd = attn_out.shape[1]
+    slots = write_pos.shape[1]
+    depth = out_proj_t.shape[0]
+    bw, lw, nz = depth // n, half // n, n // 4
+    nq = nz
+    rwt = read_weights.T
+    gate = jnp.pad(memory_gate.T, ((0, 0), (0, lw - slots)))
+    wpos = jnp.tile(write_pos, (1, 3))
+    V = pltpu.VMEM
+    D = pltpu.SemaphoreType.DMA
+    vmem = pl.BlockSpec(memory_space=pltpu.VMEM)
+    return pl.pallas_call(
+        functools.partial(kernel, n),
+        out_shape=(
+            jax.ShapeDtypeStruct((seg, hd), BF16),
+            jax.ShapeDtypeStruct((bw, hd), F32),
+            jax.ShapeDtypeStruct((slots, half), F32),
+        ),
+        in_specs=[vmem, pl.BlockSpec(memory_space=pl.ANY), vmem, vmem, vmem, vmem],
+        out_specs=(vmem, vmem, vmem),
+        scratch_shapes=[
+            V((depth, hd), BF16),
+            V((seg, hd), BF16),
+            V((seg, half), BF16),
+            V((seg, half), BF16),
+            V((seg, half), BF16),
+            V((2 * nq, seg, bw), BF16),
+            V((seg, hd), F32),
+            V((seg, 3 * slots), BF16),
+            V((slots, half), F32),
+            V((slots, half), F32),
+            V((slots, half), F32),
+            V((n, 2 * slots, lw), F32),
+            V((n, 2 * slots, lw), F32),
+            V((n, 2 * slots, lw), F32),
+            V((n, 2 * slots, lw), F32),
+            V((nq, bw, hd), BF16),
+            V((nq, bw, hd), BF16),
+            V((nq, bw, hd), F32),
+            V((nq, bw, hd), BF16),
+            V((nz, bw, hd), BF16),
+            V((bw, hd), F32),
+            D,
+            D((2 * nq,)),
+            D((2 * nq,)),
+            D((n,)),
+            D((n,)),
+            D((n,)),
+            D((n,)),
+            D,
+            D,
+            D,
+            D,
+            D((2 * nq,)),
+            D((2 * nq,)),
+            D((nq,)),
+            D((nq,)),
+            D((nq,)),
+            D((nz,)),
+        ],
+        compiler_params=pltpu.CompilerParams(
+            collective_id=0, has_side_effects=True, vmem_limit_bytes=62 * 1024 * 1024
+        ),
+    )(attn_out, out_proj_t, grad_out, rwt, gate, wpos)
+
+
+def plain(attn_out, out_proj_t, grad_out, read_weights, memory_gate, write_pos):
     high = lax.Precision.HIGHEST
     seg_len = attn_out.shape[0]
     slots = write_pos.shape[1]
@@ -43,6 +370,22 @@
 
 
 def solution(mesh):
+    n = mesh.shape["dp"]
+    parts = mesh.shape["tensor"]
+
+    def body(attn_out, out_proj_t, grad_out, read_weights, memory_gate, write_pos):
+        half, hd = grad_out.shape[1], attn_out.shape[1]
+        fits = (
+            parts == 2
+            and n % 8 == 0
+            and half % (n * 128) == 0
+            and half % 256 == 0
+            and hd % 256 == 0
+            and out_proj_t.shape[0] <= 4096
+        )
+        args = (attn_out, out_proj_t, grad_out, read_weights, memory_gate, write_pos)
+        return fused(n, *args) if fits else plain(*args)
+
     return jax.shard_map(
         body,
         mesh=mesh,

time: 358 us -> 132 us (0.37); the launches traced: 354 us -> 132 us
  waiting for transfers between devices: 265 us -> 0 us
  Pallas kernels: 0 us -> 124 us
  matrix products: 54.3 us -> 0 us
  blocking collectives: 17.8 us -> 0 us
  between operations: 13.8 us -> 0.65 us
  local copies, waits for them, and re-layouts: 1.83 us -> 7.06 us
    reduce_scatter x1 -> x0, waiting for transfers between devices: 162 us -> none  [body(): grad_weight = lax.psum_scatter(term, 'dp', scatter_dimension=0, tiled=True)]
    pallas_call x0 -> x1, Pallas kernels: none -> 124 us  [fused(): pl.pallas_call(functools.partial(kernel, n), out_shape=(jax.ShapeDtypeStr...]
    all_gather x2 -> x0, waiting for transfers between devices: 103 us -> none  [the longest x1 79.9 us: body(): full_z = lax.all_gather(grad_z, 'tensor', axis=1, tiled=True)]
    dot_general x21 -> x0, matrix products: 54.3 us -> none  [the longest x16 18.7 us: sweep(): jnp.dot(gate, carry, precision=high, preferred_element_type=jnp.float32)]
    all_gather x1 -> x0, blocking collectives: 17.8 us -> none  [body(): lax.all_gather(gate_at_step, 'dp', axis=0, tiled=True)]
  transfers between devices with their start and end apart: 3 -> 0, of which waited for: 3 -> 0; matrix products, arithmetic and copies ran while one was open for 4% -> 0% of each run, Pallas kernels for 0% -> 0%
where the time goes in v1:
time: 132 us
  Pallas kernels  124 us (94%)
  local copies, waits for them, and re-layouts  7.06 us (5%)
    pallas_call x1, Pallas kernels, fused(): pl.pallas_call(functools.partial(kernel, n), out_shape=(jax.ShapeDtypeStr...  124 us
    unnamed x8, local copies, waits for them, and re-layouts  5.2 us

profile of v1, /device:TPU:25, one launch (start us, length us, event | category | flops | bytes accessed | tf_op | source)
XLA Modules:
  0.0 132.2 jit_solution(6798593866887390167)
XLA Ops:
  0.6 0.7 tile.12
  1.3 0.6 tile.13.wpos
  1.9 0.8 copy.9
  2.6 0.6 pad.4.gate
  3.3 124.5 %shard_map.85 = (bf16[768,1024]{1,0:T(8,128)(2,1)}, f32[256,1024]{1,0:T(8,128)}, f32[16,2048]{1,0:T(8,128)}) custom-call(bf16[768,1024]{1,0:T(8,128)(2,1)} %attn.1, bf16[4096,1024]{1,0:T(8,128)(2,1)} %w_hbm.1, bf16[768,2048]{1,0:T(8,128)(2,1)} %g.1, f32[16,768]{1,0:T(8,128)} %bitcast.3, f32[16,128]{1,0:T(8,128)} %pad.4.gate, s32[1,48]{1,0:T(1,128)} %tile.13.wpos), custom_call_target="tpu_custom_call" | custom-call | tf_op jit(solution)/shard_map/pallas_call | solution.py:279
  127.7 0.0 copy-start
  127.8 2.8 %copy.13 = bf16[768,1024]{1,0:T(8,128)(2,1)} copy(bf16[768,1024]{1,0:T(8,128)(2,1)} %get-tuple-element.6) | data formatting | bytes 3145728
  130.5 0.0 copy-done
  130.5 0.0 copy-start.1
  130.5 1.0 copy.14
  131.5 0.1 copy-done.1
  131.5 0.7 copy.15
Async XLA Ops:
  127.7 2.8 %copy-start = (f32[256,1024]{1,0:T(8,128)S(1)}, f32[256,1024]{1,0:T(8,128)}, u32[]{:S(2)}) copy-start(f32[256,1024]{1,0:T(8,128)} %get-tuple-element.7) | copy-start | bytes 3145732
  130.5 1.0 copy-start.1

commit v2 on v1

--- a/solution.py
+++ b/solution.py
@@ -25,10 +25,10 @@
 
 
 def kernel(
-    n, attn, w_hbm, g, rwt, gate, wpos, out_attn, out_w, out_mem,
-    w, attn_p, gx, za, zb, zp, acc, onehot, local, after, after_x,
-    lsend, lrecv, asend, arecv, ysend, yrecv, kept, zsend, zrecv, mine,
-    w_sem, x_s, x_r, l_s, l_r, a_s, a_r, ax_s, ax_r, t_s, t_r, p_s, p_r, y_s, y_r, z_s, z_r,
+    n, attn_hbm, w_hbm, g_hbm, rw, gate, wpos, out_attn, out_w, out_mem,
+    g, attn, w, attn_p, gx, za, zb, zp, acc, onehot, local, after, after_x,
+    lsend, lrecv, asend, arecv, ysend, yrecv, kept, zsend, zrecv, mine, gpad,
+    g_sem, attn_sem, w_sem, x_s, x_r, l_s, l_r, a_s, a_r, ax_s, ax_r, t_s, t_r, p_s, p_r, y_s, y_r, z_s, z_r,
 ):
     d = lax.axis_index("dp")
     t = lax.axis_index("tensor")
@@ -38,11 +38,13 @@
     nz = n // 4
     seg, half = g.shape
     hd = attn.shape[1]
-    slots = rwt.shape[0]
+    slots = rw.shape[1]
     bw = 2 * half // n
     lw = half // n
     zh = nz // 2
-    nq = 2 * zh
+    sub = 128
+    ns = bw // sub
+    nu = 2 * zh * ns
     partner = (d + 1 - 2 * c, t)
     xpeer = (d, 1 - t)
     ypeer = (d + 2 - 4 * y, t)
@@ -61,36 +63,41 @@
         pl.semaphore_signal(barrier, inc=1, device_id=(peer(o), t), device_id_type=MESH)
     pl.semaphore_signal(barrier, inc=1, device_id=xpeer, device_id_type=MESH)
 
+    gcopy = pltpu.make_async_copy(g_hbm, g, g_sem)
+    gcopy.start()
+    attncopy = pltpu.make_async_copy(attn_hbm, attn, attn_sem)
+    attncopy.start()
+    pl.semaphore_wait(barrier, n)
+
+    def place(h, u):
+        r = u // (2 * ns)
+        zz = r + h * (zh - 1 - 2 * r)
+        yd = 1 - y if (u // ns) % 2 == 0 else y
+        return zz, 2 * zz + yd, u % ns
+
+    def cols(h, u, par):
+        _, j, piece = place(h, u)
+        return pl.ds(pl.multiple_of((2 * j + par) * bw + piece * sub, sub), sub)
+
+    xcopies = []
+    for u in range(nu):
+        for k in range(2):
+            at = cols(t, u, 1 - c if k == 0 else c)
+            i = 2 * u + k
+            xcopies.append(remote(g_hbm.at[:, at], gx.at[:, at], x_s.at[i], x_r.at[i], xpeer))
+    early = 5
+    for copy in xcopies[:early]:
+        copy.start()
     wcopy = pltpu.make_async_copy(w_hbm, w, w_sem)
     wcopy.start()
-    pl.semaphore_wait(barrier, n)
-
-    def place(q):
-        zz = q // 2
-        yd = 1 - y if q % 2 == 0 else y
-        return zz, yd, 2 * zz + yd
-
-    def cols(q, par):
-        return pl.ds(pl.multiple_of((2 * place(q)[2] + par) * bw, bw), bw)
-
-    def pair_cols(q):
-        return pl.ds(pl.multiple_of(2 * place(q)[2] * bw, 2 * bw), 2 * bw)
-
-    xcopies = []
-    for q in range(nq):
-        for k in range(2):
-            par = 1 - c if k == 0 else c
-            i = 2 * q + k
-            xcopies.append(
-                remote(g.at[:, cols(q, par)], gx.at[:, cols(q, par)], x_s.at[i], x_r.at[i], xpeer)
-            )
-    early = 3
-    for copy in xcopies[:early]:
-        copy.start()
-    tcopy = remote(attn, attn_p, t_s, t_r, partner)
+    tcopy = remote(attn_hbm, attn_p, t_s, t_r, partner)
     tcopy.start()
 
-    three = split3(rwt[...])
+    three = split3(rw[...].T)
+    gpad[...] = jnp.zeros_like(gpad)
+    gpad[:, :slots] = gate[...].T
+    gcopy.wait()
+    attncopy.wait()
 
     def local_step(i, _):
         at = pl.ds(pl.multiple_of(i * tile, tile), tile)
@@ -104,17 +111,18 @@
         return local[:, pl.ds(pl.multiple_of(peer(o) * lw, lw), lw)]
 
     lrecv[0, :slots, :] = msg(0)
-    lrecv[0, slots:, :] = gate[...]
+    lrecv[0, slots:, :] = gpad[...]
     lcopies = []
     for o in range(1, n):
         lsend[o, :slots, :] = msg(o)
-        lsend[o, slots:, :] = gate[...]
+        lsend[o, slots:, :] = gpad[...]
         lcopies.append(remote(lsend.at[o], lrecv.at[o], l_s.at[o], l_r.at[o], (peer(o), t)))
     for copy in lcopies:
         copy.start()
 
     place_of = lax.broadcasted_iota(jnp.int32, (seg, 3 * slots), 0)
-    onehot[...] = jnp.where(place_of == wpos[...], 1.0, 0.0).astype(BF16)
+    wide = jnp.concatenate([wpos[...]] * 3, axis=1)
+    onehot[...] = jnp.where(place_of == wide, 1.0, 0.0).astype(BF16)
     for copy in lcopies:
         copy.wait_recv()
 
@@ -155,62 +163,76 @@
 
     pcopies = []
 
-    def to_partner(zr, q, i):
-        copy = remote(zr.at[:, cols(q, 1 - c)], zp.at[i], p_s.at[i], p_r.at[i], partner)
+    def to_partner(zr, h, u, i):
+        copy = remote(zr.at[:, cols(h, u, 1 - c)], zp.at[i], p_s.at[i], p_r.at[i], partner)
         copy.start()
         pcopies.append(copy)
 
     ncopies = []
     ycopies = {}
 
-    def grad_block(zr, q, i, first):
+    def is_other(u):
+        return (u // ns) % 2 == 0
+
+    def slot_of(u, i):
+        return (i // nu) * (nu // 2) + (u // (2 * ns)) * ns + u % ns
+
+    def grad_block(zr, h, u, i, first):
         pcopies[i].wait_recv()
         if first:
             tcopy.wait_recv()
-        slot = i // 2
+        slot = slot_of(u, i)
 
         def step(m, _):
             at = pl.ds(pl.multiple_of(m * tile, tile), tile)
-            r = tdot(zr[:, cols(q, c)], attn[:, at]) + tdot(zp[i], attn_p[:, at])
-            if q % 2 == 0:
+            r = tdot(zr[:, cols(h, u, c)], attn[:, at]) + tdot(zp[i], attn_p[:, at])
+            if is_other(u):
                 ysend[slot, :, at] = r.astype(BF16)
             else:
                 kept[slot, :, at] = r
             return 0
 
         lax.fori_loop(0, hd // tile, step, 0)
-        if q % 2 == 0:
+        if is_other(u):
             copy = remote(ysend.at[slot], yrecv.at[slot], y_s.at[slot], y_r.at[slot], ypeer)
             copy.start()
             ycopies[slot] = copy
 
-    def to_owner(h, q, i):
-        slot = i // 2
-        zd = zh * h + place(q)[0]
+    def to_owner(h, u, i):
+        slot = slot_of(u, i)
+        piece = u % ns
+        zd = zh * h + place(h, u)[0]
         ycopies[slot].wait_recv()
         own = zd == z
 
         @pl.when(own)
         def _():
-            mine[...] = kept[slot] + yrecv[slot].astype(F32)
+            mine[piece] = kept[slot] + yrecv[slot].astype(F32)
 
         @pl.when(jnp.logical_not(own))
         def _():
             o = lax.rem(zd - z + nz, nz)
             zsend[slot] = (kept[slot] + yrecv[slot].astype(F32)).astype(BF16)
             remote(
-                zsend.at[slot], zrecv.at[o], z_s.at[slot], z_r.at[o], (zd * 4 + 2 * y + c, t)
+                zsend.at[slot],
+                zrecv.at[o, piece],
+                z_s.at[slot],
+                z_r.at[o, piece],
+                (zd * 4 + 2 * y + c, t),
             ).start()
 
-        ncopies.append((own, slot, zd))
-
-    for q in range(nq):
-        fix(g, after, za, cols(q, 1 - c))
-        to_partner(za, q, q)
-        fix(g, after, za, cols(q, c))
-    for q in range(nq):
-        grad_block(za, q, q, q == 0)
+        ncopies.append((own, slot))
+
+    for u in range(nu):
+        fix(g, after, za, cols(t, u, 1 - c))
+        to_partner(za, t, u, u)
+        fix(g, after, za, cols(t, u, c))
+    for u in range(nu):
+        grad_block(za, t, u, u, u == 0)
     wcopy.wait()
+    for u in range(2 * ns):
+        if not is_other(u):
+            to_owner(t, u, u)
 
     def own_step(m, _):
         at = pl.ds(pl.multiple_of(m * tile, tile), tile)
@@ -219,48 +241,58 @@
         return 0
 
     lax.fori_loop(0, hd // tile, own_step, 0)
-    for q in range(1, nq, 2):
-        to_owner(t, q, q)
-
+    for u in range(2 * ns, nu):
+        if not is_other(u):
+            to_owner(t, u, u)
+
+    oh = 1 - t
     axcopy.wait_recv()
-    for q in range(nq):
-        i = nq + q
-        xcopies[2 * q].wait_recv()
-        fix(gx, after_x, zb, cols(q, 1 - c))
-        to_partner(zb, q, i)
-        xcopies[2 * q + 1].wait_recv()
-        fix(gx, after_x, zb, cols(q, c))
-        grad_block(zb, q, i, False)
-
-        def other_step(m, _, q=q):
-            at = pl.ds(pl.multiple_of(m * tile, tile), tile)
-            rows = pl.ds(
-                pl.multiple_of((1 - t) * half + 2 * place(q)[2] * bw, 2 * bw), 2 * bw
-            )
-            r = acc[:, at] + jnp.dot(zb[:, pair_cols(q)], w[rows, at], preferred_element_type=F32)
-            if q == nq - 1:
-                out_attn[:, at] = r.astype(BF16)
-            else:
-                acc[:, at] = r
-            return 0
-
-        if q % 2 == 1:
-            to_owner(1 - t, q, i)
-        lax.fori_loop(0, hd // tile, other_step, 0)
-
-    total = mine[...]
-    for o in range(1, nz):
-        remote(zrecv.at[o], zrecv.at[o], z_s.at[0], z_r.at[o], ypeer).wait_recv()
-        total = total + zrecv[o].astype(F32)
-    out_w[...] = total
+    for u in range(nu):
+        i = nu + u
+        xcopies[2 * u].wait_recv()
+        fix(gx, after_x, zb, cols(oh, u, 1 - c))
+        to_partner(zb, oh, u, i)
+        xcopies[2 * u + 1].wait_recv()
+        fix(gx, after_x, zb, cols(oh, u, c))
+        grad_block(zb, oh, u, i, False)
+        if not is_other(u):
+            to_owner(oh, u, i)
+
+        if (u + 1) % ns == 0:
+            wide_at = pl.multiple_of(2 * place(oh, u)[1] * bw, 2 * bw)
+
+            def other_step(m, _, wide_at=wide_at, last=u == nu - 1):
+                at = pl.ds(pl.multiple_of(m * tile, tile), tile)
+                rows = pl.ds(pl.multiple_of(oh * half + wide_at, 2 * bw), 2 * bw)
+                r = acc[:, at] + jnp.dot(
+                    zb[:, pl.ds(wide_at, 2 * bw)], w[rows, at], preferred_element_type=F32
+                )
+                if last:
+                    out_attn[:, at] = r.astype(BF16)
+                else:
+                    acc[:, at] = r
+                return 0
+
+            lax.fori_loop(0, hd // tile, other_step, 0)
+
+    for piece in range(ns):
+        total = mine[piece]
+        for o in range(1, nz):
+            remote(
+                zrecv.at[o, piece], zrecv.at[o, piece], z_s.at[0], z_r.at[o, piece], ypeer
+            ).wait_recv()
+            total = total + zrecv[o, piece].astype(F32)
+        out_w[pl.ds(piece * sub, sub), :] = total
 
     for copy in xcopies + [tcopy, axcopy] + lcopies + acopies + pcopies + list(ycopies.values()):
         copy.wait_send()
-    for own, slot, zd in ncopies:
+    for own, slot in ncopies:
 
         @pl.when(jnp.logical_not(own))
         def _():
-            remote(zsend.at[slot], zrecv.at[0], z_s.at[slot], z_r.at[0], ypeer).wait_send()
+            remote(
+                zsend.at[slot], zrecv.at[0, 0], z_s.at[slot], z_r.at[0, 0], ypeer
+            ).wait_send()
 
 
 def fused(n, attn_out, out_proj_t, grad_out, read_weights, memory_gate, write_pos):
@@ -269,10 +301,9 @@
     slots = write_pos.shape[1]
     depth = out_proj_t.shape[0]
     bw, lw, nz = depth // n, half // n, n // 4
-    nq = nz
-    rwt = read_weights.T
-    gate = jnp.pad(memory_gate.T, ((0, 0), (0, lw - slots)))
-    wpos = jnp.tile(write_pos, (1, 3))
+    sub = 128
+    ns = bw // sub
+    nu = nz * ns
     V = pltpu.VMEM
     D = pltpu.SemaphoreType.DMA
     vmem = pl.BlockSpec(memory_space=pltpu.VMEM)
@@ -283,15 +314,17 @@
             jax.ShapeDtypeStruct((bw, hd), F32),
             jax.ShapeDtypeStruct((slots, half), F32),
         ),
-        in_specs=[vmem, pl.BlockSpec(memory_space=pl.ANY), vmem, vmem, vmem, vmem],
+        in_specs=[pl.BlockSpec(memory_space=pl.ANY)] * 3 + [vmem] * 3,
         out_specs=(vmem, vmem, vmem),
         scratch_shapes=[
+            V((seg, half), BF16),
+            V((seg, hd), BF16),
             V((depth, hd), BF16),
             V((seg, hd), BF16),
             V((seg, half), BF16),
             V((seg, half), BF16),
             V((seg, half), BF16),
-            V((2 * nq, seg, bw), BF16),
+            V((2 * nu, seg, sub), BF16),
             V((seg, hd), F32),
             V((seg, 3 * slots), BF16),
             V((slots, half), F32),
@@ -301,15 +334,18 @@
             V((n, 2 * slots, lw), F32),
             V((n, 2 * slots, lw), F32),
             V((n, 2 * slots, lw), F32),
-            V((nq, bw, hd), BF16),
-            V((nq, bw, hd), BF16),
-            V((nq, bw, hd), F32),
-            V((nq, bw, hd), BF16),
-            V((nz, bw, hd), BF16),
-            V((bw, hd), F32),
-            D,
-            D((2 * nq,)),
-            D((2 * nq,)),
+            V((nu, sub, hd), BF16),
+            V((nu, sub, hd), BF16),
+            V((nu, sub, hd), F32),
+            V((nu, sub, hd), BF16),
+            V((nz, ns, sub, hd), BF16),
+            V((ns, sub, hd), F32),
+            V((slots, lw), F32),
+            D,
+            D,
+            D,
+            D((2 * nu,)),
+            D((2 * nu,)),
             D((n,)),
             D((n,)),
             D((n,)),
@@ -318,17 +354,17 @@
             D,
             D,
             D,
-            D((2 * nq,)),
-            D((2 * nq,)),
-            D((nq,)),
-            D((nq,)),
-            D((nq,)),
-            D((nz,)),
+            D((2 * nu,)),
+            D((2 * nu,)),
+            D((nu,)),
+            D((nu,)),
+            D((nu,)),
+            D((nz, ns)),
         ],
         compiler_params=pltpu.CompilerParams(
             collective_id=0, has_side_effects=True, vmem_limit_bytes=62 * 1024 * 1024
         ),
-    )(attn_out, out_proj_t, grad_out, rwt, gate, wpos)
+    )(attn_out, out_proj_t, grad_out, read_weights, memory_gate, write_pos)
 
 
 def plain(attn_out, out_proj_t, grad_out, read_weights, memory_gate, write_pos):

time: 132 us -> 120 us (0.909)
  the two profiles are of different devices: /device:TPU:25 before, /device:TPU:11 now
where the time goes in v2:
time: 120 us; the launch traced here: 119 us
  Pallas kernels  112 us (93%)
  local copies, waits for them, and re-layouts  6.15 us (5%)
    pallas_call x1, Pallas kernels, fused(): pl.pallas_call(functools.partial(kernel, n), out_shape=(jax.ShapeDtypeStr...  112 us
    unnamed x8, local copies, waits for them, and re-layouts  6.15 us

profile of v2, /device:TPU:11, one launch (start us, length us, event | category | flops | bytes accessed | tf_op | source)
XLA Modules:
  0.0 119.3 jit_solution(6739034429923217847)
XLA Ops:
  0.6 1.7 %copy.9.rw = f32[768,16]{1,0:T(8,128)} copy(f32[768,16]{0,1:T(8,128)} %param.9) | data formatting | bytes 98304 | tf_op args[3]
  2.3 112.5 %shard_map.85 = (bf16[768,1024]{1,0:T(8,128)(2,1)}, f32[256,1024]{1,0:T(8,128)}, f32[16,2048]{1,0:T(8,128)}) custom-call(bf16[768,1024]{1,0:T(8,128)(2,1)} %attn_hbm.1, bf16[4096,1024]{1,0:T(8,128)(2,1)} %w_hbm.1, bf16[768,2048]{1,0:T(8,128)(2,1)} %g_hbm.1, f32[768,16]{1,0:T(8,128)} %copy.9.rw, f32[16,16]{1,0:T(8,128)} %gate.1, s32[1,16]{1,0:T(1,128)} %wpos.1), custom_call_target="tpu_custom_call" | custom-call | tf_op jit(solution)/shard_map/pallas_call | solution.py:310
  114.8 0.0 copy-start
  114.9 2.8 %copy.13 = bf16[768,1024]{1,0:T(8,128)(2,1)} copy(bf16[768,1024]{1,0:T(8,128)(2,1)} %get-tuple-element.6) | data formatting | bytes 3145728
  117.6 0.0 copy-done
  117.6 0.0 copy-start.1
  117.6 1.0 copy.14
  118.6 0.1 copy-done.1
  118.6 0.7 copy.15
Async XLA Ops:
  114.8 2.8 %copy-start = (f32[256,1024]{1,0:T(8,128)S(1)}, f32[256,1024]{1,0:T(8,128)}, u32[]{:S(2)}) copy-start(f32[256,1024]{1,0:T(8,128)} %get-tuple-element.7) | copy-start | bytes 3145732
  117.6 1.0 copy-start.1
